TPU v7x, 32 devices: a whole 2x2x4 slice. The times are simulated.
32 devices in a mesh: cfg: 2 (over x), seq: 8 (over z, y), dp: 2 (over core).
Axes of the slice: x: 2, y: 2, z: 4, core: 2. Of those that a mesh axis runs over, the one named last changes fastest.
Arguments:
- teacher_query: bfloat16 [2, 2, 2, 1024, 2048], P('cfg', None, 'dp', 'seq'), may hold values from -6 to 6
- teacher_key: bfloat16 [2, 2, 2, 1024, 2048], P('cfg', None, 'dp', 'seq'), may hold values from -6 to 6
- teacher_value: bfloat16 [2, 2, 2, 1024, 2048], P('cfg', None, 'dp', 'seq'), may hold values from -6 to 6
- hidden: bfloat16 [2, 2, 1024, 3072], P('cfg', 'dp', 'seq'), may hold values from -6 to 6
- adapter_down_weight: bfloat16 [3, 3072, 128], replicated, may hold values from -0.109375 to 0.109375
- adapter_up_weight: bfloat16 [3, 128, 2048], replicated, may hold values from -0.5 to 0.5
- guidance_index: int32 [2, 2], P(None, 'dp'), may hold values from 0 to 7
- timestep_index: int32 [2, 2], P(None, 'dp'), may hold values from 0 to 999
Outputs:
- student_out: bfloat16 [2, 2, 1024, 2048], P('cfg', 'dp', 'seq')
- grad_down: float32 [3, 3072, 128], P(None, ('cfg', 'seq', 'dp'))
- grad_up: float32 [3, 128, 2048], P(None, ('cfg', 'dp'), 'seq')
All inputs are finite; a program needn't handle non-finite values.
Results may differ from a plain program's by a relative error of at most 0.02.
The roundings to bfloat16 on the way count: a program that leaves them out, or rounds other values in their place, can miss the bound.
Values may be sent and summed in bfloat16 or wider, within the bound.
A program may use at most 128 MiB of HBM per device.

v0:
```python
import math
import jax
import jax.numpy as jnp
from jax import lax
from jax.sharding import PartitionSpec as P

HDIM = 128
ADAPTER_RANK = 128
TSTEPS = 1000


def passed_along(value, axis, steps):
    count = lax.axis_size(axis)
    leading, last = (max(0, -steps), min(count, count - steps))
    return lax.ppermute(value, axis, [(source, source + steps) for source in range(leading, last)])


def head_probs(query_block, key_heads, factor):
    scores = (
        jnp.einsum("qhd,khd->hqk", query_block, key_heads, preferred_element_type=jnp.float32)
        * factor
    )
    highest = jnp.max(scores, axis=-1, keepdims=True)
    raised = jnp.exp(scores - highest)
    return raised / jnp.sum(raised, axis=-1, keepdims=True)


def attention_forward(queries, keys, values):
    length, columns_all = queries.shape
    heads_here = columns_all // HDIM
    factor = HDIM ** (-0.5)
    step_rows = min(512, length)
    key_heads = keys.reshape(length, heads_here, HDIM)
    value_heads = values.reshape(length, heads_here, HDIM)
    query_blocks = queries.reshape(length // step_rows, step_rows, heads_here, HDIM)

    def one_block(query_block):
        weights = head_probs(query_block, key_heads, factor).astype(jnp.bfloat16)
        return jnp.einsum("hqk,khd->qhd", weights, value_heads, preferred_element_type=jnp.float32)

    return lax.map(one_block, query_blocks).reshape(length, columns_all)


def attention_backward(queries, keys, values, upstream):
    length, columns_all = queries.shape
    heads_here = columns_all // HDIM
    factor = HDIM ** (-0.5)
    step_rows = min(512, length)
    key_heads = keys.reshape(length, heads_here, HDIM)
    value_heads = values.reshape(length, heads_here, HDIM)
    query_blocks = queries.reshape(length // step_rows, step_rows, heads_here, HDIM)
    upstream_blocks = upstream.reshape(length // step_rows, step_rows, heads_here, HDIM)

    def one_block(running, block_pair):
        key_grad, value_grad = running
        query_block, upstream_block = block_pair
        probability = head_probs(query_block, key_heads, factor)
        weights = probability.astype(jnp.bfloat16)
        value_grad = value_grad + jnp.einsum(
            "hqk,qhd->khd", weights, upstream_block, preferred_element_type=jnp.float32
        )
        prob_grad = jnp.einsum(
            "qhd,khd->hqk", upstream_block, value_heads, preferred_element_type=jnp.float32
        )
        center = jnp.sum(probability * prob_grad, axis=-1, keepdims=True)
        score_grad = (probability * (prob_grad - center)).astype(jnp.bfloat16)
        query_grad = (
            jnp.einsum("hqk,khd->qhd", score_grad, key_heads, preferred_element_type=jnp.float32)
            * factor
        )
        key_grad = (
            key_grad
            + jnp.einsum(
                "hqk,qhd->khd", score_grad, query_block, preferred_element_type=jnp.float32
            )
            * factor
        )
        return ((key_grad, value_grad), query_grad)

    empty_grad = jnp.zeros((length, heads_here, HDIM), jnp.float32)
    (key_grad, value_grad), query_grad = lax.scan(
        one_block, (empty_grad, empty_grad), (query_blocks, upstream_blocks)
    )
    return (
        query_grad.reshape(length, columns_all).astype(jnp.bfloat16),
        key_grad.reshape(length, columns_all).astype(jnp.bfloat16),
        value_grad.reshape(length, columns_all).astype(jnp.bfloat16),
    )


def body(
    teacher_query,
    teacher_key,
    teacher_value,
    hidden,
    adapter_down_weight,
    adapter_up_weight,
    guidance_index,
    timestep_index,
):
    cfg_index = lax.axis_index("cfg")
    seq_count = lax.axis_size("seq")
    tok_here = hidden.shape[2]
    total_rows = 2 * lax.axis_size("dp") * tok_here * seq_count
    input_features = hidden[0, 0]
    half_cols = input_features.shape[1] // (2 * seq_count)
    split_view = input_features.reshape(tok_here, 2, seq_count, half_cols)
    column_block = lax.all_to_all(split_view, "seq", split_axis=2, concat_axis=0, tiled=True)
    column_block = column_block.reshape(tok_here * seq_count, 2 * half_cols)
    own_pass = (teacher_query[0, :, 0], teacher_key[0, :, 0], teacher_value[0, :, 0])
    teacher_heads = (
        lax.all_to_all(own_pass[0], "seq", split_axis=2, concat_axis=1, tiled=True),
        lax.all_to_all(own_pass[1], "seq", split_axis=2, concat_axis=1, tiled=True),
        lax.all_to_all(own_pass[2], "seq", split_axis=2, concat_axis=1, tiled=True),
    )
    teacher_local = jnp.stack(
        [
            attention_forward(
                teacher_heads[0][half_index],
                teacher_heads[1][half_index],
                teacher_heads[2][half_index],
            )
            for half_index in range(2)
        ]
    )
    teacher_tokens = lax.all_to_all(
        teacher_local.astype(jnp.bfloat16), "seq", split_axis=1, concat_axis=2, tiled=True
    )
    guide_scale = 1.0 + 0.5 * guidance_index[:, 0].astype(jnp.float32)
    time_frac = (timestep_index[:, 0].astype(jnp.float32) + 0.5) / TSTEPS
    own_scale = lax.dynamic_index_in_dim(guide_scale, cfg_index, 0, keepdims=False)
    own_time = lax.dynamic_index_in_dim(time_frac, cfg_index, 0, keepdims=False)
    weighting = jnp.where(cfg_index == 0, guide_scale, 1.0 - guide_scale)
    weighted = weighting[:, None, None] * teacher_tokens.astype(jnp.float32)
    target = lax.psum_scatter(
        weighted.astype(jnp.bfloat16), "cfg", scatter_dimension=0, tiled=True
    ).astype(jnp.float32)[0]
    rank_index = jnp.arange(1, ADAPTER_RANK + 1).astype(jnp.float32)
    feature_modulation = 1.0 + 0.5 * jnp.cos(
        math.pi * rank_index * own_time + 0.25 * rank_index * own_scale
    )
    rank_projected = (
        jnp.einsum(
            "cl,elj->ecj", input_features, adapter_down_weight, preferred_element_type=jnp.float32
        )
        * feature_modulation
    ).astype(jnp.bfloat16)
    partner = passed_along(
        (teacher_query[0, 1, 0], teacher_key[0, 1, 0], teacher_value[0, 1, 0]), "cfg", 1
    )
    projected = []
    for stack_member in range(3):
        frozen = jnp.where(cfg_index == 0, own_pass[stack_member][0], partner[stack_member])
        adapted_output = jnp.dot(
            rank_projected[stack_member],
            adapter_up_weight[stack_member],
            preferred_element_type=jnp.float32,
        )
        projected.append((frozen.astype(jnp.float32) + adapted_output).astype(jnp.bfloat16))
    student = (
        lax.all_to_all(projected[0], "seq", split_axis=1, concat_axis=0, tiled=True),
        lax.all_to_all(projected[1], "seq", split_axis=1, concat_axis=0, tiled=True),
        lax.all_to_all(projected[2], "seq", split_axis=1, concat_axis=0, tiled=True),
    )
    student_local = attention_forward(student[0], student[1], student[2]).astype(jnp.bfloat16)
    student_tokens = lax.all_to_all(student_local, "seq", split_axis=0, concat_axis=1, tiled=True)
    upstream = (
        (student_tokens.astype(jnp.float32) - target) * (1.0 / math.sqrt(total_rows))
    ).astype(jnp.bfloat16)
    upstream_heads = lax.all_to_all(upstream, "seq", split_axis=1, concat_axis=0, tiled=True)
    grads_heads = attention_backward(student[0], student[1], student[2], upstream_heads)
    grads_tokens = (
        lax.all_to_all(grads_heads[0], "seq", split_axis=0, concat_axis=1, tiled=True),
        lax.all_to_all(grads_heads[1], "seq", split_axis=0, concat_axis=1, tiled=True),
        lax.all_to_all(grads_heads[2], "seq", split_axis=0, concat_axis=1, tiled=True),
    )
    gradient_stack = jnp.stack(grads_tokens)
    rank_backward = jnp.einsum(
        "sli,smi->slm", gradient_stack, adapter_up_weight, preferred_element_type=jnp.float32
    )
    up_partial = jnp.einsum(
        "ktr,ktc->krc", rank_projected, gradient_stack, preferred_element_type=jnp.float32
    )
    per_seq = lax.psum_scatter(
        up_partial.astype(jnp.bfloat16), "seq", scatter_dimension=2, tiled=True
    )
    grad_up = lax.psum_scatter(per_seq, ("cfg", "dp"), scatter_dimension=1, tiled=True).astype(
        jnp.float32
    )
    low_grad = (rank_backward * feature_modulation).astype(jnp.bfloat16)
    grad_rows = lax.all_gather(low_grad, "seq", axis=1, tiled=True)
    column_partial = jnp.einsum(
        "tc,ktr->kcr", column_block, grad_rows, preferred_element_type=jnp.float32
    )
    grad_down = lax.psum_scatter(
        column_partial.astype(jnp.bfloat16), ("cfg", "dp"), scatter_dimension=1, tiled=True
    ).astype(jnp.float32)
    return (student_tokens[None, None], grad_down, grad_up)


def solution(mesh):
    placed = (
        P("cfg", None, "dp", "seq", None),
        P("cfg", None, "dp", "seq", None),
        P("cfg", None, "dp", "seq", None),
        P("cfg", "dp", "seq", None),
        P(),
        P(),
        P(None, "dp"),
        P(None, "dp"),
    )
    return jax.shard_map(
        body,
        mesh=mesh,
        in_specs=placed,
        out_specs=(
            P("cfg", "dp", "seq", None),
            P(None, ("cfg", "seq", "dp"), None),
            P(None, ("cfg", "dp"), "seq"),
        ),
        check_vma=False,
    )
```

profile of v0, /device:TPU:0, one launch (start us, length us, event | category | flops | bytes accessed | tf_op | source)
XLA Modules:
  0.0 490.0 jit_solution(14562616477603965680)
XLA Ops:
  7.2 3.8 copy.104
  11.0 7.3 %all-to-all-start.5 = ((bf16[2,128,2048]{1,0,2:T(2,128)(2,1)}), bf16[2,128,2048]{1,0,2:T(2,128)(2,1)}, u32[]{:S(2)}, u32[]{:S(2)}) async-start(bf16[2,128,2048]{1,0,2:T(2,128)(2,1)} %bitcast.305), calls=%async_computation.5 | async-start | bytes 2097152 | tf_op jit(solution)/shard_map/all_to_all | solution.py:113
  22.0 22.2 %all-to-all-done.5 = bf16[2,128,2048]{1,0,2:T(2,128)(2,1)} async-done(((bf16[2,128,2048]{1,0,2:T(2,128)(2,1)}), bf16[2,128,2048]{1,0,2:T(2,128)(2,1)}, u32[]{:S(2)}, u32[]{:S(2)}) %all-to-all-start.5) | async-done | bytes 1048608 | tf_op jit(solution)/shard_map/all_to_all | solution.py:113
  44.2 4.2 all-to-all-start.6
  49.3 4.2 collective-permute-start.1
  61.2 12.8 %all-to-all-done.6 = bf16[2,128,2048]{1,0,2:T(2,128)(2,1)} async-done(((bf16[2,128,2048]{1,0,2:T(2,128)(2,1)}), bf16[2,128,2048]{1,0,2:T(2,128)(2,1)}, u32[]{:S(2)}, u32[]{:S(2)}) %all-to-all-start.6) | async-done | bytes 1048608 | tf_op jit(solution)/shard_map/all_to_all | solution.py:114
  74.0 4.3 all-to-all-start.4
  80.2 4.2 collective-permute-start
  92.4 11.4 %all-to-all-done.4 = bf16[2,128,2048]{1,0,2:T(2,128)(2,1)} async-done(((bf16[2,128,2048]{1,0,2:T(2,128)(2,1)}), bf16[2,128,2048]{1,0,2:T(2,128)(2,1)}, u32[]{:S(2)}, u32[]{:S(2)}) %all-to-all-start.4) | async-done | bytes 1048608 | tf_op jit(solution)/shard_map/all_to_all | solution.py:112
  121.8 5.4 %all-to-all-start.2 = ((bf16[128,8,256]{0,2,1:T(8,128)(2,1)}), bf16[128,8,256]{0,2,1:T(8,128)(2,1)S(1)}, u32[]{:S(2)}, u32[]{:S(2)}) async-start(bf16[128,8,256]{0,2,1:T(8,128)(2,1)} %bitcast.28), calls=%async_computation.2 | async-start | bytes 1048576 | tf_op jit(solution)/shard_map/all_to_all | solution.py:163
  127.2 15.5 %while.46 = (s32[]{:T(128)}, bf16[2,512,2,128]{3,1,2,0:T(8,128)(2,1)S(1)}, bf16[2,512,2,128]{3,2,1,0:T(2,128)(2,1)S(1)}, bf16[1024,2,128]{2,0,1:T(8,128)(2,1)}, bf16[1024,2,128]{2,0,1:T(8,128)(2,1)}, /*index=5*/s32[]{:T(128)}) while((s32[]{:T(128)}, bf16[2,512,2,128]{3,1,2,0:T(8,128)(2,1)S(1)}, bf16[2,512,2,128]{3,2,1,0:T(2,128)(2,1)S(1)}, ...), condition=%wide.region_7.8_spmd, body=%wide.region_4.7_spmd.sunk | while | flops 542114816 | bytes 10756173 | solution.py:41
  127.4 4.4 fusion.182
  135.2 4.4 fusion.182
  147.4 6.0 %all-to-all-start = ((bf16[128,8,256]{2,0,1:T(8,128)(2,1)}), bf16[128,8,256]{2,0,1:T(8,128)(2,1)S(1)}, u32[]{:S(2)}, u32[]{:S(2)}) async-start(bf16[128,8,256]{2,0,1:T(8,128)(2,1)} %bitcast.251), calls=%async_computation | async-start | bytes 1048576 | tf_op jit(solution)/shard_map/all_to_all | solution.py:161
  154.3 16.8 %while.47 = (s32[]{:T(128)}, bf16[2,512,2,128]{3,1,2,0:T(8,128)(2,1)}, bf16[2,512,2,128]{3,2,1,0:T(2,128)(2,1)S(1)}, bf16[1024,2,128]{2,0,1:T(8,128)(2,1)}, bf16[1024,2,128]{2,0,1:T(8,128)(2,1)}, /*index=5*/s32[]{:T(128)}) while((s32[]{:T(128)}, bf16[2,512,2,128]{3,1,2,0:T(8,128)(2,1)}, bf16[2,512,2,128]{3,2,1,0:T(2,128)(2,1)S(1)}, ...), condition=%wide.region_11.12_spmd, body=%wide.region_8.11_spmd.sunk | while | flops 542114816 | bytes 10756681 | solution.py:41
  154.4 4.4 fusion.186
  162.8 4.4 fusion.186
  179.5 6.0 %all-to-all-start.7 = ((bf16[2,1024,256]{2,0,1:T(2,128)(2,1)}), bf16[2,1024,256]{2,0,1:T(2,128)(2,1)S(1)}, u32[]{:S(2)}, u32[]{:S(2)}) async-start(bf16[2,1024,256]{2,0,1:T(2,128)(2,1)} %copy.116), calls=%async_computation.7 | async-start | bytes 2097152 | tf_op jit(solution)/shard_map/all_to_all | solution.py:126
  189.0 21.0 %all-to-all-done.7 = bf16[2,1024,256]{2,0,1:T(2,128)(2,1)S(1)} async-done(((bf16[2,1024,256]{2,0,1:T(2,128)(2,1)}), bf16[2,1024,256]{2,0,1:T(2,128)(2,1)S(1)}, u32[]{:S(2)}, u32[]{:S(2)}) %all-to-all-start.7) | async-done | bytes 1048608 | tf_op jit(solution)/shard_map/all_to_all | solution.py:126
  215.0 13.1 %while.45 = (s32[]{:T(128)}, bf16[2,512,2,128]{3,1,2,0:T(8,128)(2,1)S(1)}, bf16[2,512,2,128]{3,1,2,0:T(8,128)(2,1)S(1)}, bf16[1024,2,128]{2,0,1:T(8,128)(2,1)S(1)}, bf16[1024,2,128]{2,0,1:T(8,128)(2,1)}, /*index=5*/s32[]{:T(128)}) while((s32[]{:T(128)}, bf16[2,512,2,128]{3,1,2,0:T(8,128)(2,1)S(1)}, bf16[2,512,2,128]{3,1,2,0:T(8,128)(2,1)S(1)}, ...), condition=%wide.region_3.4_spmd, body=%wide.region_0.3_spmd.sunk | while | flops 542114816 | bytes 12329065 | solution.py:41
  235.7 11.8 %all-to-all-done.3 = bf16[8,128,256]{2,1,0:T(8,128)(2,1)S(1)} async-done(((bf16[8,128,256]{2,1,0:T(8,128)(2,1)}), bf16[8,128,256]{2,1,0:T(8,128)(2,1)S(1)}, u32[]{:S(2)}, u32[]{:S(2)}) %all-to-all-start.3) | async-done | bytes 524320 | tf_op jit(solution)/shard_map/all_to_all | solution.py:166
  252.3 14.4 %all-to-all-done.8 = bf16[128,8,256]{2,0,1:T(8,128)(2,1)S(1)} async-done(((bf16[128,8,256]{2,0,1:T(8,128)(2,1)}), bf16[128,8,256]{2,0,1:T(8,128)(2,1)S(1)}, u32[]{:S(2)}, u32[]{:S(2)}) %all-to-all-start.8) | async-done | bytes 524320 | tf_op jit(solution)/shard_map/all_to_all | solution.py:170
  267.7 31.3 %while.48 = (s32[]{:T(128)}, f32[1024,2,128]{0,2,1:T(8,128)S(1)}, f32[1024,2,128]{0,2,1:T(8,128)}, bf16[2,512,2,128]{3,1,2,0:T(8,128)(2,1)}, bf16[2,512,2,128]{3...) while((s32[]{:T(128)}, f32[1024,2,128]{0,2,1:T(8,128)S(1)}, ...), condition=%wide.region_17.18_spmd.clone, body=%wide.region_13.17_spmd.clone.sunk | while | flops 1356201984 | bytes 79193864 | solution.py:81
  267.7 4.6 fusion.196
  282.7 4.7 fusion.196
  306.7 13.4 %all-to-all-done.9 = bf16[8,128,256]{2,1,0:T(8,128)(2,1)S(1)} async-done(((bf16[8,128,256]{2,1,0:T(8,128)(2,1)}), bf16[8,128,256]{2,1,0:T(8,128)(2,1)S(1)}, u32[]{:S(2)}, u32[]{:S(2)}) %all-to-all-start.9) | async-done | bytes 524320 | tf_op jit(solution)/shard_map/all_to_all | solution.py:173
  326.2 12.1 %all-to-all-done.10 = bf16[8,128,256]{2,1,0:T(8,128)(2,1)S(1)} async-done(((bf16[8,128,256]{2,1,0:T(8,128)(2,1)}), bf16[8,128,256]{2,1,0:T(8,128)(2,1)S(1)}, u32[]{:S(2)}, u32[]{:S(2)}) %all-to-all-start.10) | async-done | bytes 524320 | tf_op jit(solution)/shard_map/all_to_all | solution.py:174
  343.2 13.5 %all-to-all-done.11 = bf16[8,128,256]{2,1,0:T(8,128)(2,1)S(1)} async-done(((bf16[8,128,256]{2,1,0:T(8,128)(2,1)}), bf16[8,128,256]{2,1,0:T(8,128)(2,1)S(1)}, u32[]{:S(2)}, u32[]{:S(2)}) %all-to-all-start.11) | async-done | bytes 524320 | tf_op jit(solution)/shard_map/all_to_all | solution.py:175
  362.6 36.0 %all_to_all.182 = bf16[128,2,8,192]{0,3,1,2:T(8,128)(2,1)S(1)} all-to-all(bf16[128,2,8,192]{0,3,1,2:T(8,128)(2,1)S(1)} %copy.131), channel_id=1, replica_groups=mesh['cfg'=2,'seq'=8,'dp'=2] {'seq'}, dimensions={2} | all-to-all | bytes 1572864 | tf_op jit(solution)/shard_map/all_to_all | solution.py:108
  402.9 32.7 %all_gather.3 = bf16[3,1024,128]{2,1,0:T(8,128)(2,1)S(1)} all-gather(bf16[3,128,128]{2,1,0:T(8,128)(2,1)S(1)} %fusion.92), channel_id=1, replica_groups=mesh['cfg'=2,'seq'=8,'dp'=2] {'seq'}, dimensions={1}, use_global_device_ids=true | all-gather | bytes 884736 | tf_op jit(solution)/shard_map/all_gather | solution.py:191
  442.0 17.9 %reduce-scatter.13.cloned.1.call-done = bf16[96,384]{1,0:T(8,128)(2,1)} async-done(((bf16[384,384]{1,0:T(8,128)(2,1)}), bf16[96,384]{1,0:T(8,128)(2,1)}) %reduce-scatter.13.cloned.1.call-update) | async-done | bytes 73744
  461.7 20.3 %reduce-scatter.11.cloned.1.call-done = bf16[3,32,256]{2,1,0:T(8,128)(2,1)} async-done(((bf16[3,128,256]{2,1,0:T(8,128)(2,1)}), bf16[3,32,256]{2,1,0:T(8,128)(2,1)}) %reduce-scatter.11.cloned.1.call-update) | async-done | bytes 49168 | tf_op jit(solution)/shard_map/reduce_scatter | solution.py:187
  (203 shorter events, 162.3 us)
Async XLA Ops:
  7.2 79.2 %copy-start = (bf16[3,3072,128]{2,1,0:T(8,128)(2,1)S(1)}, bf16[3,3072,128]{2,1,0:T(8,128)(2,1)}, u32[]{:S(2)}) copy-start(bf16[3,3072,128]{2,1,0:T(8,128)(2,1)} %param.20) | copy-start | bytes 7077892
  7.2 41.3 %copy-start.10 = (bf16[1,2,1,128,2048]{4,3,2,1,0:T(8,128)(2,1)S(1)}, bf16[1,2,1,128,2048]{4,3,2,1,0:T(8,128)(2,1)}, u32[]{:S(2)}) copy-start(bf16[1,2,1,128,2048]{4,3,2,1,0:T(8,128)(2,1)} %param.17) | copy-start | bytes 3145732
  11.0 33.2 %all-to-all-start.5 = ((bf16[2,128,2048]{1,0,2:T(2,128)(2,1)}), bf16[2,128,2048]{1,0,2:T(2,128)(2,1)}, u32[]{:S(2)}, u32[]{:S(2)}) async-start(bf16[2,128,2048]{1,0,2:T(2,128)(2,1)} %bitcast.305), calls=%async_computation.5 | async-start | bytes 2097152 | tf_op jit(solution)/shard_map/all_to_all | solution.py:113
  44.2 29.8 %all-to-all-start.6 = ((bf16[2,128,2048]{1,0,2:T(2,128)(2,1)}), bf16[2,128,2048]{1,0,2:T(2,128)(2,1)}, u32[]{:S(2)}, u32[]{:S(2)}) async-start(bf16[2,128,2048]{1,0,2:T(2,128)(2,1)} %bitcast.304), calls=%async_computation.6 | async-start | bytes 2097152 | tf_op jit(solution)/shard_map/all_to_all | solution.py:114
  48.5 35.9 %copy-start.23 = (s32[2,1]{0,1:T(1,128)S(1)}, s32[2,1]{0,1:T(1,128)}, u32[]{:S(2)}) copy-start(s32[2,1]{0,1:T(1,128)} %param.23) | copy-start | bytes 28
  48.5 35.9 %copy-start.24 = (s32[2,1]{0,1:T(1,128)S(1)}, s32[2,1]{0,1:T(1,128)}, u32[]{:S(2)}) copy-start(s32[2,1]{0,1:T(1,128)} %param.22) | copy-start | bytes 28
  49.3 39.0 %collective-permute-start.1 = (bf16[128,2048]{1,0:T(8,128)(2,1)}, bf16[128,2048]{1,0:T(8,128)(2,1)}, u32[]{:S(2)}, u32[]{:S(2)}) collective-permute-start(bf16[128,2048]{1,0:T(8,128)(2,1)} %slice_bitcast_fusion.1), channel_id=1, source_target_pairs={{0,16},{1,17},{2,18},{3,19},{4,20},{5,21},{6,22},{7,23},{8,24},{9,... | collective-permute-start | bytes 1572872 | tf_op jit(solution)/shard_map/ppermute | solution.py:15
  55.4 35.4 %collective-permute-start.2 = (bf16[128,2048]{1,0:T(8,128)(2,1)}, bf16[128,2048]{1,0:T(8,128)(2,1)}, u32[]{:S(2)}, u32[]{:S(2)}) collective-permute-start(bf16[128,2048]{1,0:T(8,128)(2,1)} %slice_bitcast_fusion), channel_id=1, source_target_pairs={{0,16},{1,17},{2,18},{3,19},{4,20},{5,21},{6,22},{7,23},{8,24},{9,... | collective-permute-start | bytes 1572872 | tf_op jit(solution)/shard_map/ppermute | solution.py:15
  74.0 29.7 %all-to-all-start.4 = ((bf16[2,128,2048]{1,0,2:T(2,128)(2,1)}), bf16[2,128,2048]{1,0,2:T(2,128)(2,1)}, u32[]{:S(2)}, u32[]{:S(2)}) async-start(bf16[2,128,2048]{1,0,2:T(2,128)(2,1)} %bitcast.303), calls=%async_computation.4 | async-start | bytes 2097152 | tf_op jit(solution)/shard_map/all_to_all | solution.py:112
  80.2 27.0 %collective-permute-start = (bf16[128,2048]{1,0:T(8,128)(2,1)}, bf16[128,2048]{1,0:T(8,128)(2,1)}, u32[]{:S(2)}, u32[]{:S(2)}) collective-permute-start(bf16[128,2048]{1,0:T(8,128)(2,1)} %slice_bitcast_fusion.2), channel_id=1, source_target_pairs={{0,16},{1,17},{2,18},{3,19},{4,20},{5,21},{6,22},{7,23},{8,24},{9,... | collective-permute-start | bytes 1572872 | tf_op jit(solution)/shard_map/ppermute | solution.py:15
  88.3 20.3 %copy-start.15 = (bf16[3,128,128]{2,1,0:T(8,128)(2,1)}, bf16[3,128,128]{2,1,0:T(8,128)(2,1)S(1)}, u32[]{:S(2)}) copy-start(bf16[3,128,128]{2,1,0:T(8,128)(2,1)S(1)} %fusion.91) | copy-start | bytes 294916
  88.3 18.9 %copy-start.11 = (bf16[1,2,1,128,2048]{4,3,2,1,0:T(8,128)(2,1)S(1)}, bf16[1,2,1,128,2048]{4,3,2,1,0:T(8,128)(2,1)}, u32[]{:S(2)}) copy-start(bf16[1,2,1,128,2048]{4,3,2,1,0:T(8,128)(2,1)} %param.16) | copy-start | bytes 3145732
  103.7 18.0 %all-to-all-start.1 = ((bf16[128,8,256]{0,2,1:T(8,128)(2,1)}), bf16[128,8,256]{0,2,1:T(8,128)(2,1)S(1)}, u32[]{:S(2)}, u32[]{:S(2)}) async-start(bf16[128,8,256]{0,2,1:T(8,128)(2,1)} %bitcast.22), calls=%async_computation.1 | async-start | bytes 1048576 | tf_op jit(solution)/shard_map/all_to_all | solution.py:162
  121.8 25.6 %all-to-all-start.2 = ((bf16[128,8,256]{0,2,1:T(8,128)(2,1)}), bf16[128,8,256]{0,2,1:T(8,128)(2,1)S(1)}, u32[]{:S(2)}, u32[]{:S(2)}) async-start(bf16[128,8,256]{0,2,1:T(8,128)(2,1)} %bitcast.28), calls=%async_computation.2 | async-start | bytes 1048576 | tf_op jit(solution)/shard_map/all_to_all | solution.py:163
  147.4 31.4 %all-to-all-start = ((bf16[128,8,256]{2,0,1:T(8,128)(2,1)}), bf16[128,8,256]{2,0,1:T(8,128)(2,1)S(1)}, u32[]{:S(2)}, u32[]{:S(2)}) async-start(bf16[128,8,256]{2,0,1:T(8,128)(2,1)} %bitcast.251), calls=%async_computation | async-start | bytes 1048576 | tf_op jit(solution)/shard_map/all_to_all | solution.py:161
  179.5 30.4 %all-to-all-start.7 = ((bf16[2,1024,256]{2,0,1:T(2,128)(2,1)}), bf16[2,1024,256]{2,0,1:T(2,128)(2,1)S(1)}, u32[]{:S(2)}, u32[]{:S(2)}) async-start(bf16[2,1024,256]{2,0,1:T(2,128)(2,1)} %copy.116), calls=%async_computation.7 | async-start | bytes 2097152 | tf_op jit(solution)/shard_map/all_to_all | solution.py:126
  185.5 48.9 %reduce-scatter.7.cloned.1.call-start = ((), (), s32[]{:S(2)}) async-start(), calls=%async_computation.17 | async-start | bytes 1572864 | tf_op jit(solution)/shard_map/reduce_scatter | solution.py:135
  228.2 20.3 %copy-start.5 = (bf16[2,512,2,128]{3,1,2,0:T(8,128)(2,1)}, bf16[2,512,2,128]{3,1,2,0:T(8,128)(2,1)S(1)}, u32[]{:S(2)}) copy-start(bf16[2,512,2,128]{3,1,2,0:T(8,128)(2,1)S(1)} %get-tuple-element.556) | copy-start | bytes 1572868
  228.7 39.0 %copy-start.19 = (bf16[1024,2,128]{2,0,1:T(8,128)(2,1)S(1)}, bf16[1024,2,128]{2,0,1:T(8,128)(2,1)}, u32[]{:S(2)}) copy-start(bf16[1024,2,128]{2,0,1:T(8,128)(2,1)} %get-tuple-element.580) | copy-start | bytes 1572868
  229.9 17.7 %all-to-all-start.3 = ((bf16[8,128,256]{2,1,0:T(8,128)(2,1)}), bf16[8,128,256]{2,1,0:T(8,128)(2,1)S(1)}, u32[]{:S(2)}, u32[]{:S(2)}) async-start(bf16[8,128,256]{2,1,0:T(8,128)(2,1)} %convert_element_type.143), calls=%async_computation.3 | async-start | bytes 1048576 | tf_op jit(solution)/shard_map/all_to_all | solution.py:166
  247.5 19.1 %copy-start.8 = (bf16[8,128,256]{2,1,0:T(8,128)(2,1)}, bf16[8,128,256]{2,1,0:T(8,128)(2,1)S(1)}, u32[]{:S(2)}) copy-start(bf16[8,128,256]{2,1,0:T(8,128)(2,1)S(1)} %all-to-all-done.3) | copy-start | bytes 1572868
  248.5 18.1 %all-to-all-start.8 = ((bf16[128,8,256]{2,0,1:T(8,128)(2,1)}), bf16[128,8,256]{2,0,1:T(8,128)(2,1)S(1)}, u32[]{:S(2)}, u32[]{:S(2)}) async-start(bf16[128,8,256]{2,0,1:T(8,128)(2,1)} %multiply_convert_fusion.1), calls=%async_computation.9 | async-start | bytes 1048576 | tf_op jit(solution)/shard_map/all_to_all | solution.py:170
  301.7 18.3 %all-to-all-start.9 = ((bf16[8,128,256]{2,1,0:T(8,128)(2,1)}), bf16[8,128,256]{2,1,0:T(8,128)(2,1)S(1)}, u32[]{:S(2)}, u32[]{:S(2)}) async-start(bf16[8,128,256]{2,1,0:T(8,128)(2,1)} %convert_element_type.152), calls=%async_computation.10 | async-start | bytes 1048576 | tf_op jit(solution)/shard_map/all_to_all | solution.py:173
  320.0 18.3 %all-to-all-start.10 = ((bf16[8,128,256]{2,1,0:T(8,128)(2,1)}), bf16[8,128,256]{2,1,0:T(8,128)(2,1)S(1)}, u32[]{:S(2)}, u32[]{:S(2)}) async-start(bf16[8,128,256]{2,1,0:T(8,128)(2,1)} %copy.144), calls=%async_computation.11 | async-start | bytes 1048576 | tf_op jit(solution)/shard_map/all_to_all | solution.py:174
  338.3 18.3 %all-to-all-start.11 = ((bf16[8,128,256]{2,1,0:T(8,128)(2,1)}), bf16[8,128,256]{2,1,0:T(8,128)(2,1)S(1)}, u32[]{:S(2)}, u32[]{:S(2)}) async-start(bf16[8,128,256]{2,1,0:T(8,128)(2,1)} %copy.145), calls=%async_computation.12 | async-start | bytes 1048576 | tf_op jit(solution)/shard_map/all_to_all | solution.py:175
  342.0 98.2 %reduce-scatter.9.cloned.1.call-start = ((), (), s32[]{:S(2)}) async-start(), calls=%async_computation.18 | async-start | bytes 1769472 | tf_op jit(solution)/shard_map/reduce_scatter | solution.py:184
  342.3 18.0 %copy-start.16 = (bf16[3,128,128]{2,1,0:T(8,128)(2,1)S(1)}, bf16[3,128,128]{2,1,0:T(8,128)(2,1)}, u32[]{:S(2)}) copy-start(bf16[3,128,128]{2,1,0:T(8,128)(2,1)} %copy-done.15) | copy-start | bytes 294916
  362.1 38.2 %copy-start.22 = (f32[128]{0:T(128)S(1)}, f32[128]{0:T(128)}, u32[]{:S(2)}) copy-start(f32[128]{0:T(128)} %copy-done.21) | copy-start | bytes 1540
  362.1 97.8 %reduce-scatter.13.cloned.1.call-start = ((), (), s32[]{:S(2)}) async-start(), calls=%async_computation.20 | async-start | bytes 368640
  400.3 40.4 %copy-start.9 = (bf16[8,128,256]{2,1,0:T(8,128)(2,1)S(1)}, bf16[8,128,256]{2,1,0:T(8,128)(2,1)}, u32[]{:S(2)}) copy-start(bf16[8,128,256]{2,1,0:T(8,128)(2,1)} %copy-done.8) | copy-start | bytes 1572868
  400.3 83.1 %copy-start.1 = (bf16[3,3072,128]{2,1,0:T(8,128)(2,1)S(1)}, bf16[3,3072,128]{2,1,0:T(8,128)(2,1)}, u32[]{:S(2)}) copy-start(bf16[3,3072,128]{2,1,0:T(8,128)(2,1)} %param.20) | copy-start | bytes 7077892
  440.1 41.9 %reduce-scatter.11.cloned.1.call-start = ((), (), s32[]{:S(2)}) async-start(), calls=%async_computation.19 | async-start | bytes 245760 | tf_op jit(solution)/shard_map/reduce_scatter | solution.py:187
  (18 other events, 62.8 us)
Sparse Core Ops, SparseCore 0:
  215.1 19.3 reduce-scatter.6
  362.2 74.5 reduce-scatter.8
  440.2 19.5 reduce-scatter.12
  462.2 19.7 reduce-scatter.10
where the time goes:
time: 493 us; the launch traced here: 490 us
  waiting for transfers between devices  173 us (35%)
  matrix products  86.5 us (18%)
  local copies, waits for them, and re-layouts  70.6 us (14%)
  blocking collectives  68.7 us (14%)
  starting transfers between devices  65.5 us (13%)
  between operations  15.7 us (3%)
  other arithmetic  9.88 us (2%)
    all_to_all x1, blocking collectives, body(): lax.all_to_all(split_view, 'seq', split_axis=2, concat_axis=0, tiled=True)  36 us
    sub x8, matrix products, head_probs(): raised = jnp.exp(scores - highest)  33.6 us
    all_gather x1, blocking collectives, body(): grad_rows = lax.all_gather(low_grad, 'seq', axis=1, tiled=True)  32.7 us
    all_to_all x1, waiting for transfers between devices, body(): lax.all_to_all(own_pass[1], 'seq', split_axis=2, concat_axis=1, tiled=True)  22.2 us
    all_to_all x1, waiting for transfers between devices, body(): lax.all_to_all(teacher_local.astype(jnp.bfloat16), 'seq', split_axis=1, c...  21 us
    reduce_scatter x1, waiting for transfers between devices, body(): lax.psum_scatter(per_seq, ('cfg', 'dp'), scatter_dimension=1, tiled=True)  20.3 us
    dot_general x6, matrix products, one_block(): jnp.einsum('hqk,khd->qhd', weights, value_heads, preferred_element_type=j...  20.2 us
    unnamed x52, local copies, waits for them, and re-layouts  18.6 us
  transfers between devices with their start and end apart: 19, of which 13 were waited for; matrix products, arithmetic and copies ran while one was open for 23% of the time, Pallas kernels for 0%

commit v1 on v0

--- a/solution.py
+++ b/solution.py
@@ -188,10 +188,27 @@
         jnp.float32
     )
     low_grad = (rank_backward * feature_modulation).astype(jnp.bfloat16)
-    grad_rows = lax.all_gather(low_grad, "seq", axis=1, tiled=True)
-    column_partial = jnp.einsum(
-        "tc,ktr->kcr", column_block, grad_rows, preferred_element_type=jnp.float32
-    )
+    peers, place = (lax.axis_size("seq"), lax.axis_index("seq"))
+    behind = [(i, (i - 1) % peers) for i in range(peers)]
+    span = low_grad.shape[1]
+    held = low_grad
+    total = jnp.einsum(
+        "tc,ktr->kcr",
+        lax.dynamic_slice_in_dim(column_block, place * span, held.shape[1], axis=0),
+        held,
+        preferred_element_type=jnp.float32,
+    )
+    for step in range(1, peers):
+        held = lax.ppermute(held, "seq", behind)
+        total = total + jnp.einsum(
+            "tc,ktr->kcr",
+            lax.dynamic_slice_in_dim(
+                column_block, (place + step) % peers * span, held.shape[1], axis=0
+            ),
+            held,
+            preferred_element_type=jnp.float32,
+        )
+    column_partial = total
     grad_down = lax.psum_scatter(
         column_partial.astype(jnp.bfloat16), ("cfg", "dp"), scatter_dimension=1, tiled=True
     ).astype(jnp.float32)

time: 493 us -> 509 us (1.032); the launches traced: 490 us -> 499 us
  blocking collectives: 68.7 us -> 0 us
  waiting for transfers between devices: 173 us -> 212 us
  starting transfers between devices: 65.5 us -> 103 us
    all_to_all x1 -> x0, blocking collectives: 36 us -> none  [body(): lax.all_to_all(split_view, 'seq', split_axis=2, concat_axis=0, tiled=True)]
    ppermute x0 -> x7, starting transfers between devices: none -> 33.2 us  [body(): held = lax.ppermute(held, 'seq', behind)]
    all_gather x1 -> x0, blocking collectives: 32.7 us -> none  [body(): grad_rows = lax.all_gather(low_grad, 'seq', axis=1, tiled=True)]
    all_to_all x0 -> x1, waiting for transfers between devices: none -> 22 us  [body(): lax.all_to_all(split_view, 'seq', split_axis=2, concat_axis=0, tiled=True)]
    ppermute x0 -> x7, waiting for transfers between devices: none -> 15.2 us  [body(): held = lax.ppermute(held, 'seq', behind)]
  transfers between devices with their start and end apart: 19 -> 27, of which waited for: 13 -> 21; matrix products, arithmetic and copies ran while one was open for 23% -> 24% of each run, Pallas kernels for 0% -> 0%
where the time goes in v1:
time: 509 us; the launch traced here: 499 us
  waiting for transfers between devices  212 us (42%)
  starting transfers between devices  103 us (20%)
  matrix products  90.1 us (18%)
  local copies, waits for them, and re-layouts  68.3 us (13%)
  between operations  16.3 us (3%)
  other arithmetic  9.83 us (2%)
    sub x8, matrix products, head_probs(): raised = jnp.exp(scores - highest)  33.6 us
    ppermute x7, starting transfers between devices, body(): held = lax.ppermute(held, 'seq', behind)  33.2 us
    all_to_all x1, waiting for transfers between devices, body(): lax.all_to_all(own_pass[1], 'seq', split_axis=2, concat_axis=1, tiled=True)  22.2 us
    all_to_all x1, waiting for transfers between devices, body(): lax.all_to_all(split_view, 'seq', split_axis=2, concat_axis=0, tiled=True)  22 us
    unnamed x5, waiting for transfers between devices  21.2 us
    all_to_all x1, waiting for transfers between devices, body(): lax.all_to_all(teacher_local.astype(jnp.bfloat16), 'seq', split_axis=1, c...  21 us
    reduce_scatter x1, waiting for transfers between devices, body(): lax.psum_scatter(per_seq, ('cfg', 'dp'), scatter_dimension=1, tiled=True)  20.3 us
    dot_general x6, matrix products, one_block(): jnp.einsum('hqk,khd->qhd', weights, value_heads, preferred_element_type=j...  20.2 us
  transfers between devices with their start and end apart: 27, of which 21 were waited for; matrix products, arithmetic and copies ran while one was open for 24% of the time, Pallas kernels for 0%

profile of v1, /device:TPU:0, one launch (start us, length us, event | category | flops | bytes accessed | tf_op | source)
XLA Modules:
  0.0 499.0 jit_solution(1226713007294597672)
XLA Ops:
  11.0 7.3 %all-to-all-start.5 = ((bf16[2,128,2048]{1,0,2:T(2,128)(2,1)}), bf16[2,128,2048]{1,0,2:T(2,128)(2,1)}, u32[]{:S(2)}, u32[]{:S(2)}) async-start(bf16[2,128,2048]{1,0,2:T(2,128)(2,1)} %bitcast.333), calls=%async_computation.5 | async-start | bytes 2097152 | tf_op jit(solution)/shard_map/all_to_all | solution.py:113
  22.0 22.2 %all-to-all-done.5 = bf16[2,128,2048]{1,0,2:T(2,128)(2,1)} async-done(((bf16[2,128,2048]{1,0,2:T(2,128)(2,1)}), bf16[2,128,2048]{1,0,2:T(2,128)(2,1)}, u32[]{:S(2)}, u32[]{:S(2)}) %all-to-all-start.5) | async-done | bytes 1048608 | tf_op jit(solution)/shard_map/all_to_all | solution.py:113
  61.2 12.8 %all-to-all-done.6 = bf16[2,128,2048]{1,0,2:T(2,128)(2,1)} async-done(((bf16[2,128,2048]{1,0,2:T(2,128)(2,1)}), bf16[2,128,2048]{1,0,2:T(2,128)(2,1)}, u32[]{:S(2)}, u32[]{:S(2)}) %all-to-all-start.6) | async-done | bytes 1048608 | tf_op jit(solution)/shard_map/all_to_all | solution.py:114
  92.3 11.4 %all-to-all-done.4 = bf16[2,128,2048]{1,0,2:T(2,128)(2,1)} async-done(((bf16[2,128,2048]{1,0,2:T(2,128)(2,1)}), bf16[2,128,2048]{1,0,2:T(2,128)(2,1)}, u32[]{:S(2)}, u32[]{:S(2)}) %all-to-all-start.4) | async-done | bytes 1048608 | tf_op jit(solution)/shard_map/all_to_all | solution.py:112
  121.8 5.4 %all-to-all-start.2 = ((bf16[128,8,256]{0,2,1:T(8,128)(2,1)}), bf16[128,8,256]{0,2,1:T(8,128)(2,1)S(1)}, u32[]{:S(2)}, u32[]{:S(2)}) async-start(bf16[128,8,256]{0,2,1:T(8,128)(2,1)} %bitcast.28), calls=%async_computation.2 | async-start | bytes 1048576 | tf_op jit(solution)/shard_map/all_to_all | solution.py:163
  127.2 15.5 %while.46 = (s32[]{:T(128)}, bf16[2,512,2,128]{3,1,2,0:T(8,128)(2,1)S(1)}, bf16[2,512,2,128]{3,2,1,0:T(2,128)(2,1)S(1)}, bf16[1024,2,128]{2,0,1:T(8,128)(2,1)}, bf16[1024,2,128]{2,0,1:T(8,128)(2,1)}, /*index=5*/s32[]{:T(128)}) while((s32[]{:T(128)}, bf16[2,512,2,128]{3,1,2,0:T(8,128)(2,1)S(1)}, bf16[2,512,2,128]{3,2,1,0:T(2,128)(2,1)S(1)}, ...), condition=%wide.region_7.8_spmd, body=%wide.region_4.7_spmd.sunk | while | flops 542114816 | bytes 10756173 | solution.py:41
  127.4 4.4 fusion.214
  135.2 4.4 fusion.214
  147.4 6.2 %all-to-all-start = ((bf16[128,8,256]{2,0,1:T(8,128)(2,1)}), bf16[128,8,256]{2,0,1:T(8,128)(2,1)S(1)}, u32[]{:S(2)}, u32[]{:S(2)}) async-start(bf16[128,8,256]{2,0,1:T(8,128)(2,1)} %bitcast.279), calls=%async_computation | async-start | bytes 1048576 | tf_op jit(solution)/shard_map/all_to_all | solution.py:161
  154.5 16.7 %while.47 = (s32[]{:T(128)}, bf16[2,512,2,128]{3,1,2,0:T(8,128)(2,1)}, bf16[2,512,2,128]{3,2,1,0:T(2,128)(2,1)S(1)}, bf16[1024,2,128]{2,0,1:T(8,128)(2,1)}, bf16[1024,2,128]{2,0,1:T(8,128)(2,1)}, /*index=5*/s32[]{:T(128)}) while((s32[]{:T(128)}, bf16[2,512,2,128]{3,1,2,0:T(8,128)(2,1)}, bf16[2,512,2,128]{3,2,1,0:T(2,128)(2,1)S(1)}, ...), condition=%wide.region_11.12_spmd, body=%wide.region_8.11_spmd.sunk | while | flops 542114816 | bytes 10756681 | solution.py:41
  154.7 4.4 fusion.218
  163.1 4.4 fusion.218
  179.9 6.0 %all-to-all-start.7 = ((bf16[2,1024,256]{2,0,1:T(2,128)(2,1)}), bf16[2,1024,256]{2,0,1:T(2,128)(2,1)S(1)}, u32[]{:S(2)}, u32[]{:S(2)}) async-start(bf16[2,1024,256]{2,0,1:T(2,128)(2,1)} %copy.153), calls=%async_computation.7 | async-start | bytes 2097152 | tf_op jit(solution)/shard_map/all_to_all | solution.py:126
  189.3 21.0 %all-to-all-done.7 = bf16[2,1024,256]{2,0,1:T(2,128)(2,1)S(1)} async-done(((bf16[2,1024,256]{2,0,1:T(2,128)(2,1)}), bf16[2,1024,256]{2,0,1:T(2,128)(2,1)S(1)}, u32[]{:S(2)}, u32[]{:S(2)}) %all-to-all-start.7) | async-done | bytes 1048608 | tf_op jit(solution)/shard_map/all_to_all | solution.py:126
  215.3 13.1 %while.45 = (s32[]{:T(128)}, bf16[2,512,2,128]{3,1,2,0:T(8,128)(2,1)S(1)}, bf16[2,512,2,128]{3,1,2,0:T(8,128)(2,1)S(1)}, bf16[1024,2,128]{2,0,1:T(8,128)(2,1)S(1)}, bf16[1024,2,128]{2,0,1:T(8,128)(2,1)}, /*index=5*/s32[]{:T(128)}) while((s32[]{:T(128)}, bf16[2,512,2,128]{3,1,2,0:T(8,128)(2,1)S(1)}, bf16[2,512,2,128]{3,1,2,0:T(8,128)(2,1)S(1)}, ...), condition=%wide.region_3.4_spmd, body=%wide.region_0.3_spmd.sunk | while | flops 542114816 | bytes 12329065 | solution.py:41
  236.0 11.8 %all-to-all-done.3 = bf16[8,128,256]{2,1,0:T(8,128)(2,1)S(1)} async-done(((bf16[8,128,256]{2,1,0:T(8,128)(2,1)}), bf16[8,128,256]{2,1,0:T(8,128)(2,1)S(1)}, u32[]{:S(2)}, u32[]{:S(2)}) %all-to-all-start.3) | async-done | bytes 524320 | tf_op jit(solution)/shard_map/all_to_all | solution.py:166
  252.7 14.5 %all-to-all-done.8 = bf16[128,8,256]{2,0,1:T(8,128)(2,1)S(1)} async-done(((bf16[128,8,256]{2,0,1:T(8,128)(2,1)}), bf16[128,8,256]{2,0,1:T(8,128)(2,1)S(1)}, u32[]{:S(2)}, u32[]{:S(2)}) %all-to-all-start.8) | async-done | bytes 524320 | tf_op jit(solution)/shard_map/all_to_all | solution.py:170
  268.2 31.2 %while.48 = (s32[]{:T(128)}, f32[1024,2,128]{0,2,1:T(8,128)S(1)}, f32[1024,2,128]{0,2,1:T(8,128)}, bf16[2,512,2,128]{3,1,2,0:T(8,128)(2,1)}, bf16[2,512,2,128]{3...) while((s32[]{:T(128)}, f32[1024,2,128]{0,2,1:T(8,128)S(1)}, ...), condition=%wide.region_17.18_spmd.clone, body=%wide.region_13.17_spmd.clone.sunk | while | flops 1356201984 | bytes 79193864 | solution.py:81
  268.2 4.6 fusion.228
  283.1 4.6 fusion.228
  307.1 13.4 %all-to-all-done.9 = bf16[8,128,256]{2,1,0:T(8,128)(2,1)S(1)} async-done(((bf16[8,128,256]{2,1,0:T(8,128)(2,1)}), bf16[8,128,256]{2,1,0:T(8,128)(2,1)S(1)}, u32[]{:S(2)}, u32[]{:S(2)}) %all-to-all-start.9) | async-done | bytes 524320 | tf_op jit(solution)/shard_map/all_to_all | solution.py:173
  326.6 12.1 %all-to-all-done.10 = bf16[8,128,256]{2,1,0:T(8,128)(2,1)S(1)} async-done(((bf16[8,128,256]{2,1,0:T(8,128)(2,1)}), bf16[8,128,256]{2,1,0:T(8,128)(2,1)S(1)}, u32[]{:S(2)}, u32[]{:S(2)}) %all-to-all-start.10) | async-done | bytes 524320 | tf_op jit(solution)/shard_map/all_to_all | solution.py:174
  344.9 12.2 %all-to-all-done.11 = bf16[8,128,256]{2,1,0:T(8,128)(2,1)S(1)} async-done(((bf16[8,128,256]{2,1,0:T(8,128)(2,1)}), bf16[8,128,256]{2,1,0:T(8,128)(2,1)S(1)}, u32[]{:S(2)}, u32[]{:S(2)}) %all-to-all-start.11) | async-done | bytes 524320 | tf_op jit(solution)/shard_map/all_to_all | solution.py:175
  363.3 22.0 %all-to-all-done.12 = bf16[128,2,8,192]{0,3,1,2:T(8,128)(2,1)S(1)} async-done(((bf16[128,2,8,192]{0,3,1,2:T(8,128)(2,1)}), bf16[128,2,8,192]{0,3,1,2:T(8,128)(2,1)S(1)}, u32[]{:S(2)}, u32[]{:S(2)}) %all-to-all-start.12) | async-done | bytes 786464 | tf_op jit(solution)/shard_map/all_to_all | solution.py:108
  396.0 5.2 %collective-permute-start.4 = (bf16[3,128,128]{2,1,0:T(8,128)(2,1)S(1)}, bf16[3,128,128]{2,1,0:T(8,128)(2,1)S(1)}, u32[]{:S(2)}, u32[]{:S(2)}) collective-permute-start(bf16[3,128,128]{2,1,0:T(8,128)(2,1)S(1)} %collective-permute-done.3), channel_id=1, source_target_pairs={{0,14},{2,0},{4,2},{6,4},{8,6},{10,8},{12,10},{14,12},{1,15},{3,1}... | collective-permute-start | bytes 294920 | tf_op jit(solution)/shard_map/ppermute | solution.py:202
  403.4 5.1 %collective-permute-start.5 = (bf16[3,128,128]{2,1,0:T(8,128)(2,1)S(1)}, bf16[3,128,128]{2,1,0:T(8,128)(2,1)S(1)}, u32[]{:S(2)}, u32[]{:S(2)}) collective-permute-start(bf16[3,128,128]{2,1,0:T(8,128)(2,1)S(1)} %collective-permute-done.4), channel_id=1, source_target_pairs={{0,14},{2,0},{4,2},{6,4},{8,6},{10,8},{12,10},{14,12},{1,15},{3,1}... | collective-permute-start | bytes 294920 | tf_op jit(solution)/shard_map/ppermute | solution.py:202
  410.7 5.1 %collective-permute-start.6 = (bf16[3,128,128]{2,1,0:T(8,128)(2,1)S(1)}, bf16[3,128,128]{2,1,0:T(8,128)(2,1)S(1)}, u32[]{:S(2)}, u32[]{:S(2)}) collective-permute-start(bf16[3,128,128]{2,1,0:T(8,128)(2,1)S(1)} %collective-permute-done.5), channel_id=1, source_target_pairs={{0,14},{2,0},{4,2},{6,4},{8,6},{10,8},{12,10},{14,12},{1,15},{3,1}... | collective-permute-start | bytes 294920 | tf_op jit(solution)/shard_map/ppermute | solution.py:202
  418.0 5.1 %collective-permute-start.7 = (bf16[3,128,128]{2,1,0:T(8,128)(2,1)S(1)}, bf16[3,128,128]{2,1,0:T(8,128)(2,1)S(1)}, u32[]{:S(2)}, u32[]{:S(2)}) collective-permute-start(bf16[3,128,128]{2,1,0:T(8,128)(2,1)S(1)} %collective-permute-done.6), channel_id=1, source_target_pairs={{0,14},{2,0},{4,2},{6,4},{8,6},{10,8},{12,10},{14,12},{1,15},{3,1}... | collective-permute-start | bytes 294920 | tf_op jit(solution)/shard_map/ppermute | solution.py:202
  425.5 5.3 %collective-permute-start.8 = (bf16[3,128,128]{2,1,0:T(8,128)(2,1)S(1)}, bf16[3,128,128]{2,1,0:T(8,128)(2,1)S(1)}, u32[]{:S(2)}, u32[]{:S(2)}) collective-permute-start(bf16[3,128,128]{2,1,0:T(8,128)(2,1)S(1)} %collective-permute-done.7), channel_id=1, source_target_pairs={{0,14},{2,0},{4,2},{6,4},{8,6},{10,8},{12,10},{14,12},{1,15},{3,1}... | collective-permute-start | bytes 294920 | tf_op jit(solution)/shard_map/ppermute | solution.py:202
  434.8 5.2 %collective-permute-start.9 = (bf16[3,128,128]{2,1,0:T(8,128)(2,1)S(1)}, bf16[3,128,128]{2,1,0:T(8,128)(2,1)S(1)}, u32[]{:S(2)}, u32[]{:S(2)}) collective-permute-start(bf16[3,128,128]{2,1,0:T(8,128)(2,1)S(1)} %collective-permute-done.8), channel_id=1, source_target_pairs={{0,14},{2,0},{4,2},{6,4},{8,6},{10,8},{12,10},{14,12},{1,15},{3,1}... | collective-permute-start | bytes 294920 | tf_op jit(solution)/shard_map/ppermute | solution.py:202
  447.9 20.6 %reduce-scatter.13.cloned.1.call-done = bf16[96,384]{1,0:T(8,128)(2,1)} async-done(((bf16[384,384]{1,0:T(8,128)(2,1)}), bf16[96,384]{1,0:T(8,128)(2,1)}) %reduce-scatter.13.cloned.1.call-update) | async-done | bytes 73744
  470.4 20.3 %reduce-scatter.11.cloned.1.call-done = bf16[3,32,256]{2,1,0:T(8,128)(2,1)} async-done(((bf16[3,128,256]{2,1,0:T(8,128)(2,1)}), bf16[3,32,256]{2,1,0:T(8,128)(2,1)}) %reduce-scatter.11.cloned.1.call-update) | async-done | bytes 49168 | tf_op jit(solution)/shard_map/reduce_scatter | solution.py:187
  (224 shorter events, 205.6 us)
Async XLA Ops:
  7.2 79.2 %copy-start = (bf16[3,3072,128]{2,1,0:T(8,128)(2,1)S(1)}, bf16[3,3072,128]{2,1,0:T(8,128)(2,1)}, u32[]{:S(2)}) copy-start(bf16[3,3072,128]{2,1,0:T(8,128)(2,1)} %param.20) | copy-start | bytes 7077892
  7.2 41.3 %copy-start.9 = (bf16[1,2,1,128,2048]{4,3,2,1,0:T(8,128)(2,1)S(1)}, bf16[1,2,1,128,2048]{4,3,2,1,0:T(8,128)(2,1)}, u32[]{:S(2)}) copy-start(bf16[1,2,1,128,2048]{4,3,2,1,0:T(8,128)(2,1)} %param.17) | copy-start | bytes 3145732
  11.0 33.2 %all-to-all-start.5 = ((bf16[2,128,2048]{1,0,2:T(2,128)(2,1)}), bf16[2,128,2048]{1,0,2:T(2,128)(2,1)}, u32[]{:S(2)}, u32[]{:S(2)}) async-start(bf16[2,128,2048]{1,0,2:T(2,128)(2,1)} %bitcast.333), calls=%async_computation.5 | async-start | bytes 2097152 | tf_op jit(solution)/shard_map/all_to_all | solution.py:113
  44.2 29.8 %all-to-all-start.6 = ((bf16[2,128,2048]{1,0,2:T(2,128)(2,1)}), bf16[2,128,2048]{1,0,2:T(2,128)(2,1)}, u32[]{:S(2)}, u32[]{:S(2)}) async-start(bf16[2,128,2048]{1,0,2:T(2,128)(2,1)} %bitcast.332), calls=%async_computation.6 | async-start | bytes 2097152 | tf_op jit(solution)/shard_map/all_to_all | solution.py:114
  49.3 39.0 %collective-permute-start.1 = (bf16[128,2048]{1,0:T(8,128)(2,1)}, bf16[128,2048]{1,0:T(8,128)(2,1)}, u32[]{:S(2)}, u32[]{:S(2)}) collective-permute-start(bf16[128,2048]{1,0:T(8,128)(2,1)} %slice_bitcast_fusion.1), channel_id=1, source_target_pairs={{0,16},{1,17},{2,18},{3,19},{4,20},{5,21},{6,22},{7,23},{8,24},{9,... | collective-permute-start | bytes 1572872 | tf_op jit(solution)/shard_map/ppermute | solution.py:15
  55.4 35.4 %collective-permute-start.2 = (bf16[128,2048]{1,0:T(8,128)(2,1)}, bf16[128,2048]{1,0:T(8,128)(2,1)}, u32[]{:S(2)}, u32[]{:S(2)}) collective-permute-start(bf16[128,2048]{1,0:T(8,128)(2,1)} %slice_bitcast_fusion), channel_id=1, source_target_pairs={{0,16},{1,17},{2,18},{3,19},{4,20},{5,21},{6,22},{7,23},{8,24},{9,... | collective-permute-start | bytes 1572872 | tf_op jit(solution)/shard_map/ppermute | solution.py:15
  74.0 29.7 %all-to-all-start.4 = ((bf16[2,128,2048]{1,0,2:T(2,128)(2,1)}), bf16[2,128,2048]{1,0,2:T(2,128)(2,1)}, u32[]{:S(2)}, u32[]{:S(2)}) async-start(bf16[2,128,2048]{1,0,2:T(2,128)(2,1)} %bitcast.331), calls=%async_computation.4 | async-start | bytes 2097152 | tf_op jit(solution)/shard_map/all_to_all | solution.py:112
  80.2 27.1 %collective-permute-start = (bf16[128,2048]{1,0:T(8,128)(2,1)}, bf16[128,2048]{1,0:T(8,128)(2,1)}, u32[]{:S(2)}, u32[]{:S(2)}) collective-permute-start(bf16[128,2048]{1,0:T(8,128)(2,1)} %slice_bitcast_fusion.2), channel_id=1, source_target_pairs={{0,16},{1,17},{2,18},{3,19},{4,20},{5,21},{6,22},{7,23},{8,24},{9,... | collective-permute-start | bytes 1572872 | tf_op jit(solution)/shard_map/ppermute | solution.py:15
  103.7 18.0 %all-to-all-start.1 = ((bf16[128,8,256]{0,2,1:T(8,128)(2,1)}), bf16[128,8,256]{0,2,1:T(8,128)(2,1)S(1)}, u32[]{:S(2)}, u32[]{:S(2)}) async-start(bf16[128,8,256]{0,2,1:T(8,128)(2,1)} %bitcast.22), calls=%async_computation.1 | async-start | bytes 1048576 | tf_op jit(solution)/shard_map/all_to_all | solution.py:162
  121.8 25.7 %all-to-all-start.2 = ((bf16[128,8,256]{0,2,1:T(8,128)(2,1)}), bf16[128,8,256]{0,2,1:T(8,128)(2,1)S(1)}, u32[]{:S(2)}, u32[]{:S(2)}) async-start(bf16[128,8,256]{0,2,1:T(8,128)(2,1)} %bitcast.28), calls=%async_computation.2 | async-start | bytes 1048576 | tf_op jit(solution)/shard_map/all_to_all | solution.py:163
  147.4 31.6 %all-to-all-start = ((bf16[128,8,256]{2,0,1:T(8,128)(2,1)}), bf16[128,8,256]{2,0,1:T(8,128)(2,1)S(1)}, u32[]{:S(2)}, u32[]{:S(2)}) async-start(bf16[128,8,256]{2,0,1:T(8,128)(2,1)} %bitcast.279), calls=%async_computation | async-start | bytes 1048576 | tf_op jit(solution)/shard_map/all_to_all | solution.py:161
  179.9 30.4 %all-to-all-start.7 = ((bf16[2,1024,256]{2,0,1:T(2,128)(2,1)}), bf16[2,1024,256]{2,0,1:T(2,128)(2,1)S(1)}, u32[]{:S(2)}, u32[]{:S(2)}) async-start(bf16[2,1024,256]{2,0,1:T(2,128)(2,1)} %copy.153), calls=%async_computation.7 | async-start | bytes 2097152 | tf_op jit(solution)/shard_map/all_to_all | solution.py:126
  185.8 48.9 %reduce-scatter.7.cloned.1.call-start = ((), (), s32[]{:S(2)}) async-start(), calls=%async_computation.17 | async-start | bytes 1572864 | tf_op jit(solution)/shard_map/reduce_scatter | solution.py:135
  229.0 39.2 %copy-start.19 = (bf16[1024,2,128]{2,0,1:T(8,128)(2,1)S(1)}, bf16[1024,2,128]{2,0,1:T(8,128)(2,1)}, u32[]{:S(2)}) copy-start(bf16[1024,2,128]{2,0,1:T(8,128)(2,1)} %get-tuple-element.581) | copy-start | bytes 1572868
  230.1 17.7 %all-to-all-start.3 = ((bf16[8,128,256]{2,1,0:T(8,128)(2,1)}), bf16[8,128,256]{2,1,0:T(8,128)(2,1)S(1)}, u32[]{:S(2)}, u32[]{:S(2)}) async-start(bf16[8,128,256]{2,1,0:T(8,128)(2,1)} %convert_element_type.140), calls=%async_computation.3 | async-start | bytes 1048576 | tf_op jit(solution)/shard_map/all_to_all | solution.py:166
  248.8 18.3 %all-to-all-start.8 = ((bf16[128,8,256]{2,0,1:T(8,128)(2,1)}), bf16[128,8,256]{2,0,1:T(8,128)(2,1)S(1)}, u32[]{:S(2)}, u32[]{:S(2)}) async-start(bf16[128,8,256]{2,0,1:T(8,128)(2,1)} %multiply_convert_fusion.1), calls=%async_computation.9 | async-start | bytes 1048576 | tf_op jit(solution)/shard_map/all_to_all | solution.py:170
  302.1 18.3 %all-to-all-start.9 = ((bf16[8,128,256]{2,1,0:T(8,128)(2,1)}), bf16[8,128,256]{2,1,0:T(8,128)(2,1)S(1)}, u32[]{:S(2)}, u32[]{:S(2)}) async-start(bf16[8,128,256]{2,1,0:T(8,128)(2,1)} %convert_element_type.149), calls=%async_computation.10 | async-start | bytes 1048576 | tf_op jit(solution)/shard_map/all_to_all | solution.py:173
  320.4 18.3 %all-to-all-start.10 = ((bf16[8,128,256]{2,1,0:T(8,128)(2,1)}), bf16[8,128,256]{2,1,0:T(8,128)(2,1)S(1)}, u32[]{:S(2)}, u32[]{:S(2)}) async-start(bf16[8,128,256]{2,1,0:T(8,128)(2,1)} %copy.201), calls=%async_computation.11 | async-start | bytes 1048576 | tf_op jit(solution)/shard_map/all_to_all | solution.py:174
  338.8 18.3 %all-to-all-start.11 = ((bf16[8,128,256]{2,1,0:T(8,128)(2,1)}), bf16[8,128,256]{2,1,0:T(8,128)(2,1)S(1)}, u32[]{:S(2)}, u32[]{:S(2)}) async-start(bf16[8,128,256]{2,1,0:T(8,128)(2,1)} %copy.202), calls=%async_computation.12 | async-start | bytes 1048576 | tf_op jit(solution)/shard_map/all_to_all | solution.py:175
  357.1 28.3 %all-to-all-start.12 = ((bf16[128,2,8,192]{0,3,1,2:T(8,128)(2,1)}), bf16[128,2,8,192]{0,3,1,2:T(8,128)(2,1)S(1)}, u32[]{:S(2)}, u32[]{:S(2)}) async-start(bf16[128,2,8,192]{0,3,1,2:T(8,128)(2,1)} %copy.168), calls=%async_computation.13 | async-start | bytes 1572864 | tf_op jit(solution)/shard_map/all_to_all | solution.py:108
  360.7 85.4 %reduce-scatter.9.cloned.1.call-start = ((), (), s32[]{:S(2)}) async-start(), calls=%async_computation.18 | async-start | bytes 1769472 | tf_op jit(solution)/shard_map/reduce_scatter | solution.py:184
  363.2 105.4 %reduce-scatter.13.cloned.1.call-start = ((), (), s32[]{:S(2)}) async-start(), calls=%async_computation.20 | async-start | bytes 368640
  389.0 6.9 %collective-permute-start.3 = (bf16[3,128,128]{2,1,0:T(8,128)(2,1)S(1)}, bf16[3,128,128]{2,1,0:T(8,128)(2,1)S(1)}, u32[]{:S(2)}, u32[]{:S(2)}) collective-permute-start(bf16[3,128,128]{2,1,0:T(8,128)(2,1)S(1)} %fusion.93), channel_id=1, source_target_pairs={{0,14},{2,0},{4,2},{6,4},{8,6},{10,8},{12,10},{14,12},{1,15},{3,1}... | collective-permute-start | bytes 294920 | tf_op jit(solution)/shard_map/ppermute | solution.py:202
  396.0 7.4 %collective-permute-start.4 = (bf16[3,128,128]{2,1,0:T(8,128)(2,1)S(1)}, bf16[3,128,128]{2,1,0:T(8,128)(2,1)S(1)}, u32[]{:S(2)}, u32[]{:S(2)}) collective-permute-start(bf16[3,128,128]{2,1,0:T(8,128)(2,1)S(1)} %collective-permute-done.3), channel_id=1, source_target_pairs={{0,14},{2,0},{4,2},{6,4},{8,6},{10,8},{12,10},{14,12},{1,15},{3,1}... | collective-permute-start | bytes 294920 | tf_op jit(solution)/shard_map/ppermute | solution.py:202
  403.4 7.3 %collective-permute-start.5 = (bf16[3,128,128]{2,1,0:T(8,128)(2,1)S(1)}, bf16[3,128,128]{2,1,0:T(8,128)(2,1)S(1)}, u32[]{:S(2)}, u32[]{:S(2)}) collective-permute-start(bf16[3,128,128]{2,1,0:T(8,128)(2,1)S(1)} %collective-permute-done.4), channel_id=1, source_target_pairs={{0,14},{2,0},{4,2},{6,4},{8,6},{10,8},{12,10},{14,12},{1,15},{3,1}... | collective-permute-start | bytes 294920 | tf_op jit(solution)/shard_map/ppermute | solution.py:202
  408.8 37.9 %copy-start.8 = (bf16[8,128,256]{2,1,0:T(8,128)(2,1)S(1)}, bf16[8,128,256]{2,1,0:T(8,128)(2,1)}, u32[]{:S(2)}) copy-start(bf16[8,128,256]{2,1,0:T(8,128)(2,1)} %copy-done.7) | copy-start | bytes 1572868
  410.7 7.3 %collective-permute-start.6 = (bf16[3,128,128]{2,1,0:T(8,128)(2,1)S(1)}, bf16[3,128,128]{2,1,0:T(8,128)(2,1)S(1)}, u32[]{:S(2)}, u32[]{:S(2)}) collective-permute-start(bf16[3,128,128]{2,1,0:T(8,128)(2,1)S(1)} %collective-permute-done.5), channel_id=1, source_target_pairs={{0,14},{2,0},{4,2},{6,4},{8,6},{10,8},{12,10},{14,12},{1,15},{3,1}... | collective-permute-start | bytes 294920 | tf_op jit(solution)/shard_map/ppermute | solution.py:202
  418.0 7.4 %collective-permute-start.7 = (bf16[3,128,128]{2,1,0:T(8,128)(2,1)S(1)}, bf16[3,128,128]{2,1,0:T(8,128)(2,1)S(1)}, u32[]{:S(2)}, u32[]{:S(2)}) collective-permute-start(bf16[3,128,128]{2,1,0:T(8,128)(2,1)S(1)} %collective-permute-done.6), channel_id=1, source_target_pairs={{0,14},{2,0},{4,2},{6,4},{8,6},{10,8},{12,10},{14,12},{1,15},{3,1}... | collective-permute-start | bytes 294920 | tf_op jit(solution)/shard_map/ppermute | solution.py:202
  423.1 69.0 %copy-start.1 = (bf16[3,3072,128]{2,1,0:T(8,128)(2,1)S(1)}, bf16[3,3072,128]{2,1,0:T(8,128)(2,1)}, u32[]{:S(2)}) copy-start(bf16[3,3072,128]{2,1,0:T(8,128)(2,1)} %param.20) | copy-start | bytes 7077892
  425.5 9.3 %collective-permute-start.8 = (bf16[3,128,128]{2,1,0:T(8,128)(2,1)S(1)}, bf16[3,128,128]{2,1,0:T(8,128)(2,1)S(1)}, u32[]{:S(2)}, u32[]{:S(2)}) collective-permute-start(bf16[3,128,128]{2,1,0:T(8,128)(2,1)S(1)} %collective-permute-done.7), channel_id=1, source_target_pairs={{0,14},{2,0},{4,2},{6,4},{8,6},{10,8},{12,10},{14,12},{1,15},{3,1}... | collective-permute-start | bytes 294920 | tf_op jit(solution)/shard_map/ppermute | solution.py:202
  434.8 7.4 %collective-permute-start.9 = (bf16[3,128,128]{2,1,0:T(8,128)(2,1)S(1)}, bf16[3,128,128]{2,1,0:T(8,128)(2,1)S(1)}, u32[]{:S(2)}, u32[]{:S(2)}) collective-permute-start(bf16[3,128,128]{2,1,0:T(8,128)(2,1)S(1)} %collective-permute-done.8), channel_id=1, source_target_pairs={{0,14},{2,0},{4,2},{6,4},{8,6},{10,8},{12,10},{14,12},{1,15},{3,1}... | collective-permute-start | bytes 294920 | tf_op jit(solution)/shard_map/ppermute | solution.py:202
  446.1 44.6 %reduce-scatter.11.cloned.1.call-start = ((), (), s32[]{:S(2)}) async-start(), calls=%async_computation.19 | async-start | bytes 245760 | tf_op jit(solution)/shard_map/reduce_scatter | solution.py:187
  (26 other events, 315.5 us)
Sparse Core Ops, SparseCore 0:
  215.3 19.3 reduce-scatter.6
  365.0 71.8 reduce-scatter.8
  446.2 22.3 reduce-scatter.12
  470.9 19.7 reduce-scatter.10
